TPU v7x, 32 devices: a whole 2x2x4 slice. The times are simulated.
32 devices in a mesh: img: 4 (over y, core), proj: 8 (over z, x).
Axes of the slice: x: 2, y: 2, z: 4, core: 2. Of those that a mesh axis runs over, the one named last changes fastest.
Arguments:
- images: bfloat16 [512, 4096], P('img'), may hold values from -48 to 48
- projections: bfloat16 [2560, 4096], P('proj'), may hold values from -6 to 6
- noise_weight: float32 [4096], replicated, may hold values from 0.02 to 0.08
- defocus: float32 [512], P('img'), may hold values from 2 to 8
- orient_count: int32 [512], P('img'), may hold values from 160 to 2560, as said below
- term_limit: int32 [512], P('img'), may hold values from 2048 to 4096
- block_plan: int32 [16], replicated, may hold values from 0 to 15, each once
Outputs:
- reconstruction: bfloat16 [2560, 4096], P('proj', 'img')
- evidence_next: float32 [512], P('img')
Inputs may be any that keep to these rules, and one draw needn't show every extreme that they name: Orientations 0 to orient_count[i] - 1 are the significant ones of image i; some image has all 2560.
All inputs are finite; a program needn't handle non-finite values.
Results may differ from a plain program's by a relative error of at most 0.018.
Values may be sent and summed in bfloat16 or wider, within the bound.
A program may use at most 64 MiB of HBM per device.

v0:
```python
import math
import jax
import jax.numpy as jnp
from jax import lax
from jax.sharding import PartitionSpec as P

F = 4096
BLOCK = 32


def contrast_table(defocus, width):
    frequency = (jnp.arange(width, dtype=jnp.float32) + 1.0) / width
    return jnp.sin(2.0 * math.pi * defocus[:, None] * frequency[None, :] + 0.1)


def image_terms(pixels, noise_weight, defocus, limits):
    width = pixels.shape[1]
    contrast = contrast_table(defocus, width)
    keep_mask = (jnp.arange(width, dtype=jnp.int32)[None, :] < limits[:, None]).astype(jnp.float32)
    values = pixels.astype(jnp.float32)
    weighted = (keep_mask * noise_weight[None, :] * contrast * values).astype(jnp.bfloat16)
    weighted_sq = (keep_mask * noise_weight[None, :] * contrast * contrast).astype(jnp.bfloat16)
    back_images = (keep_mask * contrast * values).astype(jnp.bfloat16)
    return (weighted, weighted_sq, back_images)


def slice_weight_sums(every_post, focus_all, limit_all, start, slice_width, img_count, img_rows):
    term_ids = jnp.arange(slice_width, dtype=jnp.int32) + start
    term_float = term_ids.astype(jnp.float32)
    frequency = (term_float + 1.0) / F
    contrast = jnp.sin(2.0 * math.pi * focus_all[:, None] * frequency[None, :] + 0.1)
    keep_mask = (term_float[None, :] < limit_all[:, None]).astype(jnp.float32)
    rebuilt = (keep_mask * contrast * contrast).astype(jnp.bfloat16)
    rebuilt = rebuilt.reshape(img_count, img_rows, slice_width)
    partial_value = jnp.einsum(
        "jbi,bif->bjf", every_post, rebuilt, preferred_element_type=jnp.float32
    )
    partial_value = lax.optimization_barrier(partial_value.astype(jnp.bfloat16)).astype(jnp.float32)
    return jnp.sum(partial_value, axis=0)


def shards(images, projections, noise_weight, defocus, orient_count, term_limit, block_plan):
    proj_rows = projections.shape[0]
    img_rows = images.shape[0]
    weighted, weighted_sq, back_images = image_terms(images, noise_weight, defocus, term_limit)
    proj_sq = (projections.astype(jnp.float32) * projections.astype(jnp.float32)).astype(
        jnp.bfloat16
    )
    contract = (((1,), (1,)), ((), ()))
    scores = lax.dot_general(projections, weighted, contract, preferred_element_type=jnp.float32)
    scores = scores - 0.5 * lax.dot_general(
        proj_sq, weighted_sq, contract, preferred_element_type=jnp.float32
    )
    orient_ids = lax.axis_index("proj") * proj_rows + jnp.arange(proj_rows, dtype=jnp.int32)
    significant = orient_ids[:, None] < orient_count[None, :]
    local_peak = jnp.max(jnp.where(significant, scores, -1e30), axis=0)
    row_peak = lax.pmax(local_peak, "proj")
    safe = jnp.where(significant, scores, row_peak[None, :])
    local_mass = jnp.sum(jnp.where(significant, jnp.exp(safe - row_peak[None, :]), 0.0), axis=0)
    row_mass = lax.psum(local_mass, "proj")
    log_evidence = row_peak + jnp.log(row_mass)
    posterior = jnp.where(significant, jnp.exp(scores - log_evidence[None, :]), 0.0).astype(
        jnp.bfloat16
    )
    img_count = lax.axis_size("img")
    slice_width = F // img_count
    slice_start = lax.axis_index("img") * slice_width
    limit_float = term_limit.astype(jnp.float32)
    moved_images = lax.all_to_all(back_images, "img", split_axis=1, concat_axis=0, tiled=True)
    every_post = lax.all_gather(posterior, "img", axis=1, tiled=True)
    focus_all, limit_all = (
        lax.all_gather(defocus, "img", axis=0, tiled=True),
        lax.all_gather(limit_float, "img", axis=0, tiled=True),
    )
    every_post = every_post.reshape(proj_rows, img_count, img_rows)
    moved_images = moved_images.reshape(img_count, img_rows, slice_width)
    part_images = jnp.einsum(
        "jbi,bif->bjf", every_post, moved_images, preferred_element_type=jnp.float32
    )
    part_images = lax.optimization_barrier(part_images.astype(jnp.bfloat16)).astype(jnp.float32)
    sum_images = jnp.sum(part_images, axis=0)
    sum_weights = slice_weight_sums(
        every_post, focus_all, limit_all, slice_start, slice_width, img_count, img_rows
    )
    reconstruction = (sum_images / (sum_weights + 1.0)).astype(jnp.bfloat16)
    every_evidence = lax.all_gather(log_evidence, "img", axis=0, tiled=True)
    blocks = every_evidence.reshape(-1, BLOCK)
    local_blocks = img_rows // BLOCK
    slot_ids = lax.axis_index("img") * local_blocks + jnp.arange(local_blocks, dtype=jnp.int32)
    selector = (block_plan[None, :] == slot_ids[:, None]).astype(jnp.float32)
    own_blocks = jnp.dot(selector, blocks, precision=lax.Precision.HIGHEST)
    return (reconstruction, own_blocks.reshape(img_rows))


def solution(mesh):
    placed = (P("img", None), P("proj", None), P(), P("img"), P("img"), P("img"), P())
    return jax.shard_map(
        shards, mesh=mesh, in_specs=placed, out_specs=(P("proj", "img"), P("img")), check_vma=False
    )
```

profile of v0, /device:TPU:0, one launch (start us, length us, event | category | flops | bytes accessed | tf_op | source)
XLA Modules:
  0.0 115.0 jit_solution(12315028204032979167)
XLA Ops:
  0.6 0.0 copy-start.3
  0.7 0.7 broadcast_multiply_fusion.1
  1.3 1.6 %copy.15 = bf16[128,4096]{0,1:T(8,128)(2,1)S(1)} copy(bf16[128,4096]{1,0:T(8,128)(2,1)} %param.7) | data formatting | bytes 2097152 | tf_op args[0]
  2.9 0.0 copy-done.3
  2.9 8.5 %fusion.2 = bf16[128,4096]{0,1:T(8,128)(2,1)S(1)} fusion(bf16[128,4096]{0,1:T(8,128)(2,1)S(1)} %copy.15, f32[4096]{0:T(1024)S(1)} %add_multiply_fusion, f32[128]{0:T(128)S(1)} %broadcast_multiply_fusion.1, s32[128]{0:T(128)S(1)} %copy-done.3), kind=kLoop, calls=%fused_computation.8 | loop fusion | flops 3670016 | bytes 2114560 | tf_op jit(solution)/shard_map/convert_element_type | solution.py:23
  11.4 0.0 copy-start.5
  11.4 1.3 %copy.16 = bf16[128,4,1024]{2,0,1:T(8,128)(2,1)} copy(bf16[128,4,1024]{0,2,1:T(8,128)(2,1)S(1)} %bitcast.26) | data formatting | bytes 2097152 | tf_op jit(solution)/shard_map/all_to_all | solution.py:69
  12.7 4.3 %all-to-all-start = ((bf16[128,4,1024]{2,0,1:T(8,128)(2,1)}), bf16[128,4,1024]{2,0,1:T(8,128)(2,1)S(1)}, u32[]{:S(2)}, u32[]{:S(2)}) async-start(bf16[128,4,1024]{2,0,1:T(8,128)(2,1)} %copy.16), calls=%async_computation | async-start | bytes 2097152 | tf_op jit(solution)/shard_map/all_to_all | solution.py:69
  17.0 0.0 copy-done.5
  17.0 0.0 copy-start.1
  17.0 0.0 copy-start.4
  17.1 12.5 %convolution_bitcast_fusion = f32[320,128]{1,0:T(8,128)S(1)} fusion(bf16[320,4096]{1,0:T(8,128)(2,1)} %param.8, bf16[128,4096]{0,1:T(8,128)(2,1)S(1)} %copy.15, f32[4096]{0:T(1024)S(1)} %add_multiply_fusion, f32[128]{0:T(128)S(1)} %broadcast_multiply_fusion.1, f32[4096]{0:T(1024)S(1)} %copy-done.5, s32[128]{0:T(128)S(1)} %copy-done.3), kind=kOutput, calls=%fused_computation.19 | convolution fusion | flops 339738624 | bytes 3867648 | tf_op jit(solution)/shard_map/dot_general | solution.py:50
  29.5 0.0 copy-done.1
  29.5 0.0 copy-done.4
  29.6 0.0 copy-start.6
  29.6 0.0 copy-start.2
  29.6 8.2 %fusion.32 = (f32[128]{0:T(128)S(1)}, f32[320,128]{1,0:T(8,128)S(1)}) fusion(s32[128]{0:T(128)S(1)} %copy-done.1, s32[320]{0:T(512)S(1)} %iota_add_fusion, f32[320,128]{1,0:T(8,128)S(1)} %convolution_bitcast_fusion, f32[4096]{0:T(1024)S(1)} %add_multiply_fusion, f32[128]{0:T(128)S(1)} %broadcast_multiply_fusion.1, f32[4096]{0:T(1024)S(1)} %copy-done.5, ...), kind=kOutput, calls=%fused_computation.47 | convolution fusion | flops 343351168 | bytes 2985216 | tf_op jit(solution)/shard_map/dot_general | solution.py:51
  37.7 22.6 %pmax.7 = f32[128]{0:T(128)S(1)} all-reduce(f32[128]{0:T(128)S(1)} %get-tuple-element.2), channel_id=1, replica_groups=mesh['img'=4,'proj'=8] {'proj'}, use_global_device_ids=true, to_apply=%region_1.2 | all-reduce | flops 128 | bytes 1024 | tf_op jit(solution)/shard_map/pmax | solution.py:57
  60.3 0.1 fusion.35
  60.5 17.1 %psum.7 = f32[128]{0:T(128)S(1)} all-reduce(f32[128]{0:T(128)S(1)} %fusion.35), channel_id=1, replica_groups=mesh['img'=4,'proj'=8] {'proj'}, use_global_device_ids=true, to_apply=%region_3.4 | all-reduce | flops 128 | bytes 1024 | tf_op jit(solution)/shard_map/psum | solution.py:60
  77.6 0.1 fusion.36
  77.7 5.1 %all-gather.2 = f32[4,1,128]{2,1,0:T(1,128)S(1)} all-gather(f32[1,1,128]{2,1,0:T(1,128)S(1)} %bitcast.27), channel_id=1, replica_groups=mesh['img'=4,'proj'=8] {'img'}, dimensions={0}, use_global_device_ids=true | all-gather | bytes 2560 | tf_op jit(solution)/shard_map/all_gather | solution.py:86
  82.8 0.5 broadcast.84
  83.3 0.7 reduce.3
  84.0 0.1 reshape.73
  84.0 0.0 copy-done.6
  84.0 0.2 fusion.37
  84.2 0.6 reshape.74
  84.8 5.3 %all-gather = f32[4,1,128]{2,1,0:T(1,128)S(1)} all-gather(f32[1,1,128]{2,1,0:T(1,128)S(1)} %convert_bitcast_fusion), channel_id=1, replica_groups=mesh['img'=4,'proj'=8] {'img'}, dimensions={0}, use_global_device_ids=true | all-gather | bytes 2560 | tf_op jit(solution)/shard_map/all_gather | solution.py:73
  90.1 0.0 copy-done.2
  90.1 5.0 %all-gather.1 = f32[4,1,128]{2,1,0:T(1,128)S(1)} all-gather(f32[1,1,128]{2,1,0:T(1,128)S(1)} %bitcast.30), channel_id=1, replica_groups=mesh['img'=4,'proj'=8] {'img'}, dimensions={0}, use_global_device_ids=true | all-gather | bytes 2560 | tf_op jit(solution)/shard_map/all_gather | solution.py:72
  95.2 6.3 %all_gather.12 = bf16[320,512]{1,0:T(8,128)(2,1)S(1)} all-gather(bf16[320,128]{1,0:T(8,128)(2,1)S(1)} %fusion.36), channel_id=1, replica_groups=mesh['img'=4,'proj'=8] {'img'}, dimensions={1}, use_global_device_ids=true | all-gather | bytes 409600 | tf_op jit(solution)/shard_map/all_gather | solution.py:70
  101.5 9.4 %convolution_convert_fusion = bf16[4,320,1024]{2,1,0:T(8,128)(2,1)} fusion(f32[1024]{0:T(1024)S(1)} %add_multiply_fusion.1, f32[4,128]{1,0:T(4,128)S(1)} %bitcast.29, f32[4,128]{1,0:T(4,128)S(1)} %bitcast.28, f32[1024]{0:T(1024)S(1)} %add_convert_fusion, bf16[320,512]{1,0:T(8,128)(2,1)S(1)} %all_gather.12), kind=kOutput, calls=%fused_computation.14 | convolution fusion | flops 340000768 | bytes 2961408 | tf_op jit(solution)/shard_map/jbi,bif->bjf/dot_general | solution.py:35
  110.9 0.0 all-to-all-done
  110.9 0.0 copy-start
  110.9 0.8 convolution_convert_fusion.1
  111.8 0.9 copy-done
  112.7 1.2 %convert_reduce_fusion = (f32[320,1024]{1,0:T(8,128)S(1)}, f32[320,1024]{1,0:T(8,128)S(1)}) fusion(bf16[4,320,1024]{2,1,0:T(8,128)(2,1)S(1)} %copy-done, bf16[4,320,1024]{2,1,0:T(8,128)(2,1)S(1)} %convolution_convert_fusion.1), kind=kLoop, calls=%fused_computation | loop fusion | flops 4587520 | bytes 7864320 | tf_op jit(solution)/shard_map/reduce_sum | solution.py:39
  113.9 1.1 divide_convert_fusion
  (8 shorter events, 0.0 us)
Async XLA Ops:
  0.6 2.3 %copy-start.3 = (s32[128]{0:T(128)S(1)}, s32[128]{0:T(128)}, u32[]{:S(2)}) copy-start(s32[128]{0:T(128)} %param.12) | copy-start | bytes 1540
  11.4 5.6 %copy-start.5 = (f32[4096]{0:T(1024)S(1)}, f32[4096]{0:T(1024)}, u32[]{:S(2)}) copy-start(f32[4096]{0:T(1024)} %param.9) | copy-start | bytes 49156
  12.7 98.2 %all-to-all-start = ((bf16[128,4,1024]{2,0,1:T(8,128)(2,1)}), bf16[128,4,1024]{2,0,1:T(8,128)(2,1)S(1)}, u32[]{:S(2)}, u32[]{:S(2)}) async-start(bf16[128,4,1024]{2,0,1:T(8,128)(2,1)} %copy.16), calls=%async_computation | async-start | bytes 2097152 | tf_op jit(solution)/shard_map/all_to_all | solution.py:69
  17.0 12.5 %copy-start.1 = (s32[128]{0:T(128)S(1)}, s32[128]{0:T(128)}, u32[]{:S(2)}) copy-start(s32[128]{0:T(128)} %param.11) | copy-start | bytes 1540
  17.0 12.5 %copy-start.4 = (bf16[320,4096]{1,0:T(8,128)(2,1)S(1)}, bf16[320,4096]{1,0:T(8,128)(2,1)}, u32[]{:S(2)}) copy-start(bf16[320,4096]{1,0:T(8,128)(2,1)} %param.8) | copy-start | bytes 7864324
  29.6 54.5 %copy-start.6 = (s32[16]{0:T(128)S(1)}, s32[16]{0:T(128)}, u32[]{:S(2)}) copy-start(s32[16]{0:T(128)} %param.13) | copy-start | bytes 196
  29.6 60.6 %copy-start.2 = (f32[128]{0:T(128)S(1)}, f32[128]{0:T(128)}, u32[]{:S(2)}) copy-start(f32[128]{0:T(128)} %param.10) | copy-start | bytes 1540
  110.9 1.7 %copy-start = (bf16[4,320,1024]{2,1,0:T(8,128)(2,1)S(1)}, bf16[4,320,1024]{2,1,0:T(8,128)(2,1)}, u32[]{:S(2)}) copy-start(bf16[4,320,1024]{2,1,0:T(8,128)(2,1)} %convolution_convert_fusion) | copy-start | bytes 7864324
where the time goes:
time: 115 us
  blocking collectives  61.5 us (53%)
  matrix products  31 us (27%)
  other arithmetic  12.4 us (11%)
  local copies, waits for them, and re-layouts  5.05 us (4%)
  starting transfers between devices  4.26 us (4%)
    pmax x1, blocking collectives, shards(): row_peak = lax.pmax(local_peak, 'proj')  22.6 us
    psum x1, blocking collectives, shards(): row_mass = lax.psum(local_mass, 'proj')  17.1 us
    dot_general x1, matrix products, shards(): lax.dot_general(projections, weighted, contract, preferred_element_type=j...  12.5 us
    dot_general x1, matrix products, slice_weight_sums(): jnp.einsum('jbi,bif->bjf', every_post, rebuilt, preferred_element_type=jn...  9.38 us
    convert_element_type x1, other arithmetic, image_terms(): back_images = (keep_mask * contrast * values).astype(jnp.bfloat16)  8.45 us
    dot_general x1, matrix products, shards(): lax.dot_general(proj_sq, weighted_sq, contract, preferred_element_type=jn...  8.17 us
    all_gather x1, blocking collectives, shards(): every_post = lax.all_gather(posterior, 'img', axis=1, tiled=True)  6.34 us
    all_gather x1, blocking collectives, shards(): lax.all_gather(limit_float, 'img', axis=0, tiled=True)  5.29 us
  transfers between devices with their start and end apart: 1, of which 0 were waited for; matrix products, arithmetic and copies ran while one was open for 28% of the time, Pallas kernels for 0%

commit v1 on v0

--- a/solution.py
+++ b/solution.py
@@ -6,6 +6,30 @@
 
 F = 4096
 BLOCK = 32
+
+
+def drive_the_object(row_data, where_dim):
+    z1 = list(row_data.shape[1:])
+    z1[where_dim] *= row_data.shape[0]
+    return jnp.moveaxis(row_data, 0, where_dim).reshape(z1)
+
+
+def reach_sample(xin, mesh_dim):
+    outcome_arr = lax.axis_size(mesh_dim)
+    known = lax.axis_index(mesh_dim)
+    h_now, front = (outcome_arr, known)
+    val2, value_now = (xin[None], 1)
+    while value_now < h_now:
+        all_blocks = []
+        s = 0
+        while s < h_now:
+            all_blocks.append((s, s ^ value_now))
+            s += 1
+        mat_out = lax.ppermute(val2, axis_name=mesh_dim, perm=all_blocks)
+        v_next = front & value_now == 0
+        val2 = jnp.concatenate([jnp.where(v_next, val2, mat_out), jnp.where(v_next, mat_out, val2)])
+        value_now *= 2
+    return val2
 
 
 def contrast_table(defocus, width):
@@ -67,7 +91,8 @@
     slice_start = lax.axis_index("img") * slice_width
     limit_float = term_limit.astype(jnp.float32)
     moved_images = lax.all_to_all(back_images, "img", split_axis=1, concat_axis=0, tiled=True)
-    every_post = lax.all_gather(posterior, "img", axis=1, tiled=True)
+    taken_in = reach_sample(posterior, "img")
+    every_post = drive_the_object(taken_in, 1)
     focus_all, limit_all = (
         lax.all_gather(defocus, "img", axis=0, tiled=True),
         lax.all_gather(limit_float, "img", axis=0, tiled=True),

time: 115 us -> 111 us (0.965)
  blocking collectives: 61.5 us -> 55.4 us
  starting transfers between devices: 4.26 us -> 5.98 us
    all_gather x1 -> x0, blocking collectives: 6.34 us -> none  [shards(): every_post = lax.all_gather(posterior, 'img', axis=1, tiled=True)]
    ppermute x0 -> x2, starting transfers between devices: none -> 1.72 us  [reach_sample(): mat_out = lax.ppermute(val2, axis_name=mesh_dim, perm=all_blocks)]
  transfers between devices with their start and end apart: 1 -> 3, of which waited for: 0 -> 0; matrix products, arithmetic and copies ran while one was open for 28% -> 29% of each run, Pallas kernels for 0% -> 0%
where the time goes in v1:
time: 111 us
  blocking collectives  55.4 us (50%)
  matrix products  31.3 us (28%)
  other arithmetic  12.5 us (11%)
  starting transfers between devices  5.98 us (5%)
  local copies, waits for them, and re-layouts  5.04 us (5%)
    pmax x1, blocking collectives, shards(): row_peak = lax.pmax(local_peak, 'proj')  22.6 us
    psum x1, blocking collectives, shards(): row_mass = lax.psum(local_mass, 'proj')  17.1 us
    dot_general x1, matrix products, shards(): lax.dot_general(projections, weighted, contract, preferred_element_type=j...  12.5 us
    dot_general x1, matrix products, slice_weight_sums(): jnp.einsum('jbi,bif->bjf', every_post, rebuilt, preferred_element_type=jn...  9.59 us
    convert_element_type x1, other arithmetic, image_terms(): back_images = (keep_mask * contrast * values).astype(jnp.bfloat16)  8.45 us
    dot_general x1, matrix products, shards(): lax.dot_general(proj_sq, weighted_sq, contract, preferred_element_type=jn...  8.17 us
    all_gather x1, blocking collectives, shards(): lax.all_gather(defocus, 'img', axis=0, tiled=True)  5.44 us
    all_gather x1, blocking collectives, shards(): lax.all_gather(limit_float, 'img', axis=0, tiled=True)  5.18 us
  transfers between devices with their start and end apart: 3, of which 0 were waited for; matrix products, arithmetic and copies ran while one was open for 29% of the time, Pallas kernels for 0%

profile of v1, /device:TPU:0, one launch (start us, length us, event | category | flops | bytes accessed | tf_op | source)
XLA Modules:
  0.0 111.0 jit_solution(11227211934711128961)
XLA Ops:
  0.6 0.0 copy-start.3
  0.7 0.7 broadcast_multiply_fusion.1
  1.3 1.6 %copy.11 = bf16[128,4096]{0,1:T(8,128)(2,1)S(1)} copy(bf16[128,4096]{1,0:T(8,128)(2,1)} %param.7) | data formatting | bytes 2097152 | tf_op args[0]
  2.9 0.0 copy-done.3
  2.9 8.5 %fusion.2 = bf16[128,4096]{0,1:T(8,128)(2,1)S(1)} fusion(bf16[128,4096]{0,1:T(8,128)(2,1)S(1)} %copy.11, f32[4096]{0:T(1024)S(1)} %add_multiply_fusion, f32[128]{0:T(128)S(1)} %broadcast_multiply_fusion.1, s32[128]{0:T(128)S(1)} %copy-done.3), kind=kLoop, calls=%fused_computation.8 | loop fusion | flops 3670016 | bytes 2114560 | tf_op jit(solution)/shard_map/convert_element_type | solution.py:47
  11.4 0.0 copy-start.5
  11.4 1.3 %copy.12 = bf16[128,4,1024]{2,0,1:T(8,128)(2,1)} copy(bf16[128,4,1024]{0,2,1:T(8,128)(2,1)S(1)} %bitcast.22) | data formatting | bytes 2097152 | tf_op jit(solution)/shard_map/all_to_all | solution.py:93
  12.7 4.3 %all-to-all-start = ((bf16[128,4,1024]{2,0,1:T(8,128)(2,1)}), bf16[128,4,1024]{2,0,1:T(8,128)(2,1)S(1)}, u32[]{:S(2)}, u32[]{:S(2)}) async-start(bf16[128,4,1024]{2,0,1:T(8,128)(2,1)} %copy.12), calls=%async_computation | async-start | bytes 2097152 | tf_op jit(solution)/shard_map/all_to_all | solution.py:93
  17.0 0.0 copy-done.5
  17.0 0.0 copy-start.1
  17.0 0.0 copy-start.4
  17.0 12.5 %convolution_bitcast_fusion = f32[320,128]{1,0:T(8,128)S(1)} fusion(bf16[320,4096]{1,0:T(8,128)(2,1)} %param.8, bf16[128,4096]{0,1:T(8,128)(2,1)S(1)} %copy.11, f32[4096]{0:T(1024)S(1)} %add_multiply_fusion, f32[128]{0:T(128)S(1)} %broadcast_multiply_fusion.1, f32[4096]{0:T(1024)S(1)} %copy-done.5, s32[128]{0:T(128)S(1)} %copy-done.3), kind=kOutput, calls=%fused_computation.19 | convolution fusion | flops 339738624 | bytes 3867648 | tf_op jit(solution)/shard_map/dot_general | solution.py:74
  29.5 0.0 copy-done.1
  29.5 0.0 copy-done.4
  29.5 0.0 copy-start.2
  29.6 0.0 copy-start.6
  29.6 8.2 %fusion.28 = (f32[128]{0:T(128)S(1)}, f32[320,128]{1,0:T(8,128)S(1)}) fusion(s32[128]{0:T(128)S(1)} %copy-done.1, s32[320]{0:T(512)S(1)} %iota_add_fusion, f32[320,128]{1,0:T(8,128)S(1)} %convolution_bitcast_fusion, f32[4096]{0:T(1024)S(1)} %add_multiply_fusion, f32[128]{0:T(128)S(1)} %broadcast_multiply_fusion.1, f32[4096]{0:T(1024)S(1)} %copy-done.5, ...), kind=kOutput, calls=%fused_computation.44 | convolution fusion | flops 343351168 | bytes 2985216 | tf_op jit(solution)/shard_map/dot_general | solution.py:75
  37.7 22.6 %pmax.7 = f32[128]{0:T(128)S(1)} all-reduce(f32[128]{0:T(128)S(1)} %get-tuple-element.6), channel_id=1, replica_groups=mesh['img'=4,'proj'=8] {'proj'}, use_global_device_ids=true, to_apply=%region_1.2 | all-reduce | flops 128 | bytes 1024 | tf_op jit(solution)/shard_map/pmax | solution.py:81
  60.3 0.1 fusion.31
  60.4 17.1 %psum.7 = f32[128]{0:T(128)S(1)} all-reduce(f32[128]{0:T(128)S(1)} %fusion.31), channel_id=1, replica_groups=mesh['img'=4,'proj'=8] {'proj'}, use_global_device_ids=true, to_apply=%region_3.4 | all-reduce | flops 128 | bytes 1024 | tf_op jit(solution)/shard_map/psum | solution.py:84
  77.6 0.1 fusion.33
  77.7 0.1 collective-permute-start
  77.8 0.0 copy-done.2
  77.8 5.4 %all-gather.1 = f32[4,1,128]{2,1,0:T(1,128)S(1)} all-gather(f32[1,1,128]{2,1,0:T(1,128)S(1)} %bitcast.26), channel_id=1, replica_groups=mesh['img'=4,'proj'=8] {'img'}, dimensions={0}, use_global_device_ids=true | all-gather | bytes 2560 | tf_op jit(solution)/shard_map/all_gather | solution.py:97
  83.3 5.0 %all-gather.2 = f32[4,1,128]{2,1,0:T(1,128)S(1)} all-gather(f32[1,1,128]{2,1,0:T(1,128)S(1)} %bitcast.23), channel_id=1, replica_groups=mesh['img'=4,'proj'=8] {'img'}, dimensions={0}, use_global_device_ids=true | all-gather | bytes 2560 | tf_op jit(solution)/shard_map/all_gather | solution.py:111
  88.3 0.5 broadcast.84
  88.8 0.7 reduce.3
  89.5 0.1 reshape.69
  89.6 0.0 copy-done.6
  89.6 0.2 fusion.34
  89.8 0.0 collective-permute-done
  89.8 0.1 broadcast_select_fusion.3
  89.9 1.6 %collective-permute-start.1 = (bf16[2,320,128]{2,1,0:T(8,128)(2,1)S(1)}, bf16[2,320,128]{2,1,0:T(8,128)(2,1)S(1)}, u32[]{:S(2)}, u32[]{:S(2)}) collective-permute-start(bf16[2,320,128]{2,1,0:T(8,128)(2,1)S(1)} %pad_maximum_fusion), channel_id=1, source_target_pairs={{0,16},{8,24},{16,0},{24,8},{1,17},{9,25},{17,1},{25,9},{2,18},{10... | collective-permute-start | bytes 491528 | tf_op jit(solution)/shard_map/ppermute | solution.py:28
  91.6 0.6 reshape.70
  92.2 5.2 %all-gather = f32[4,1,128]{2,1,0:T(1,128)S(1)} all-gather(f32[1,1,128]{2,1,0:T(1,128)S(1)} %convert_bitcast_fusion), channel_id=1, replica_groups=mesh['img'=4,'proj'=8] {'img'}, dimensions={0}, use_global_device_ids=true | all-gather | bytes 2560 | tf_op jit(solution)/shard_map/all_gather | solution.py:98
  97.3 0.0 collective-permute-done.1
  97.4 9.6 %convolution_convert_fusion = bf16[4,320,1024]{2,1,0:T(8,128)(2,1)} fusion(f32[1024]{0:T(1024)S(1)} %add_multiply_fusion.1, f32[4,128]{1,0:T(4,128)S(1)} %bitcast.25, f32[4,128]{1,0:T(4,128)S(1)} %bitcast.24, f32[1024]{0:T(1024)S(1)} %add_convert_fusion, bf16[2,320,128]{2,1,0:T(8,128)(2,1)S(1)} %get-tuple-element.3, ...), kind=kOutput, calls=%fused_computation.14 | convolution fusion | flops 340164608 | bytes 2961408 | tf_op jit(solution)/shard_map/jbi,bif->bjf/dot_general | solution.py:59
  107.0 0.0 all-to-all-done
  107.0 0.0 copy-start
  107.0 0.8 convolution_convert_fusion.1
  107.8 0.9 copy-done
  108.7 1.2 %convert_reduce_fusion = (f32[320,1024]{1,0:T(8,128)S(1)}, f32[320,1024]{1,0:T(8,128)S(1)}) fusion(bf16[4,320,1024]{2,1,0:T(8,128)(2,1)S(1)} %copy-done, bf16[4,320,1024]{2,1,0:T(8,128)(2,1)S(1)} %convolution_convert_fusion.1), kind=kLoop, calls=%fused_computation | loop fusion | flops 4587520 | bytes 7864320 | tf_op jit(solution)/shard_map/reduce_sum | solution.py:63
  109.9 1.1 divide_convert_fusion
  (10 shorter events, 0.1 us)
Async XLA Ops:
  0.6 2.3 %copy-start.3 = (s32[128]{0:T(128)S(1)}, s32[128]{0:T(128)}, u32[]{:S(2)}) copy-start(s32[128]{0:T(128)} %param.12) | copy-start | bytes 1540
  11.4 5.6 %copy-start.5 = (f32[4096]{0:T(1024)S(1)}, f32[4096]{0:T(1024)}, u32[]{:S(2)}) copy-start(f32[4096]{0:T(1024)} %param.9) | copy-start | bytes 49156
  12.7 94.2 %all-to-all-start = ((bf16[128,4,1024]{2,0,1:T(8,128)(2,1)}), bf16[128,4,1024]{2,0,1:T(8,128)(2,1)S(1)}, u32[]{:S(2)}, u32[]{:S(2)}) async-start(bf16[128,4,1024]{2,0,1:T(8,128)(2,1)} %copy.12), calls=%async_computation | async-start | bytes 2097152 | tf_op jit(solution)/shard_map/all_to_all | solution.py:93
  17.0 12.5 %copy-start.1 = (s32[128]{0:T(128)S(1)}, s32[128]{0:T(128)}, u32[]{:S(2)}) copy-start(s32[128]{0:T(128)} %param.11) | copy-start | bytes 1540
  17.0 12.5 %copy-start.4 = (bf16[320,4096]{1,0:T(8,128)(2,1)S(1)}, bf16[320,4096]{1,0:T(8,128)(2,1)}, u32[]{:S(2)}) copy-start(bf16[320,4096]{1,0:T(8,128)(2,1)} %param.8) | copy-start | bytes 7864324
  29.5 48.3 %copy-start.2 = (f32[128]{0:T(128)S(1)}, f32[128]{0:T(128)}, u32[]{:S(2)}) copy-start(f32[128]{0:T(128)} %param.10) | copy-start | bytes 1540
  29.6 60.0 %copy-start.6 = (s32[16]{0:T(128)S(1)}, s32[16]{0:T(128)}, u32[]{:S(2)}) copy-start(s32[16]{0:T(128)} %param.13) | copy-start | bytes 196
  77.7 12.0 %collective-permute-start = (bf16[1,320,128]{2,1,0:T(8,128)(2,1)S(1)}, bf16[1,320,128]{2,1,0:T(8,128)(2,1)S(1)}, u32[]{:S(2)}, u32[]{:S(2)}) collective-permute-start(bf16[1,320,128]{2,1,0:T(8,128)(2,1)S(1)} %fusion.33), channel_id=1, source_target_pairs={{0,8},{8,0},{16,24},{24,16},{1,9},{9,1},{17,25},{25,17},{2,10},{10... | collective-permute-start | bytes 245768 | tf_op jit(solution)/shard_map/ppermute | solution.py:28
  89.9 7.4 %collective-permute-start.1 = (bf16[2,320,128]{2,1,0:T(8,128)(2,1)S(1)}, bf16[2,320,128]{2,1,0:T(8,128)(2,1)S(1)}, u32[]{:S(2)}, u32[]{:S(2)}) collective-permute-start(bf16[2,320,128]{2,1,0:T(8,128)(2,1)S(1)} %pad_maximum_fusion), channel_id=1, source_target_pairs={{0,16},{8,24},{16,0},{24,8},{1,17},{9,25},{17,1},{25,9},{2,18},{10... | collective-permute-start | bytes 491528 | tf_op jit(solution)/shard_map/ppermute | solution.py:28
  107.0 1.7 %copy-start = (bf16[4,320,1024]{2,1,0:T(8,128)(2,1)S(1)}, bf16[4,320,1024]{2,1,0:T(8,128)(2,1)}, u32[]{:S(2)}) copy-start(bf16[4,320,1024]{2,1,0:T(8,128)(2,1)} %convolution_convert_fusion) | copy-start | bytes 7864324
